TPU v7x, 32 devices: a whole 2x2x4 slice. The times are simulated.
32 devices in a mesh: path: 8 (over z, x), tm: 4 (over y, core).
Axes of the slice: x: 2, y: 2, z: 4, core: 2. Of those that a mesh axis runs over, the one named last changes fastest.
Arguments:
- values: bfloat16 [128, 128, 8192], P('path', 'tm'), may hold values from -6 to 6
- trade_set: int32 [8192], replicated, may hold values from 0 to 1023
- lag_dates: int32 [1024], replicated, may hold values from 1 to 4
- threshold_cents: int32 [1024], replicated, may hold values from 200 to 1599
- cap_cents: int32 [1024], replicated, may hold values from 200 to 1599
Outputs:
- epe: float32 [128, 1024], P('tm')
- ene: float32 [128, 1024], P('tm')
All inputs are finite; a program needn't handle non-finite values.
Results may differ from a plain program's by a relative error of at most 0.001.
Values may be sent and summed in bfloat16 or wider, within the bound.
A program may use at most 64 MiB of HBM per device.

v0:
```python
import jax
import jax.numpy as jnp
from jax import lax
from jax.sharding import PartitionSpec as P

LAG_MAX = 4


def passed_along(value, axis, steps):
    count = lax.axis_size(axis)
    first, last = (max(0, -steps), min(count, count - steps))
    return lax.ppermute(value, axis, [(source, source + steps) for source in range(first, last)])


def entering(x, axis, combine, identity):
    devices, here = (lax.axis_size(axis), lax.axis_index(axis))
    everything = jax.tree.map(
        lambda part, kind: lax.all_gather(part.astype(kind), axis),
        x,
        jax.tree.map(lambda a: jnp.bfloat16 if a.dtype == jnp.float32 else a.dtype, x),
    )
    start = jax.tree.map(
        lambda part, zero: jnp.broadcast_to(jnp.asarray(zero, part.dtype), part.shape), x, identity
    )

    def lap(k, before):
        reached = k < here
        new = combine(
            before, jax.tree.map(lambda part, own: part[k].astype(own.dtype), everything, x)
        )
        return jax.tree.map(lambda a, b: jnp.where(reached, a, b), new, before)

    return lax.fori_loop(0, devices, lap, start)


def membership(trade_set, set_count):
    set_ids = jnp.arange(set_count, dtype=jnp.int32)[None, :]
    return (trade_set[:, None] == set_ids).astype(jnp.bfloat16)


def compose(earlier, later):
    shift_sum = earlier[0] + later[0]
    low_edge = jnp.minimum(jnp.maximum(earlier[1] + later[0], later[1]), later[2])
    high_edge = jnp.minimum(jnp.maximum(earlier[2] + later[0], later[1]), later[2])
    return (shift_sum, low_edge, high_edge)


def moves_list(date_list, lag_dates, date_rows):
    lag_masks = [(lag_dates == offset).astype(jnp.float32) for offset in range(1, LAG_MAX + 1)]
    lagged = []
    for index in range(date_rows + 1):
        total = lag_masks[0] * date_list[LAG_MAX - 1 + index]
        for offset in range(2, LAG_MAX + 1):
            total = total + lag_masks[offset - 1] * date_list[LAG_MAX - offset + index]
        lagged.append(total)
    return [lagged[index + 1] - lagged[index] for index in range(date_rows)]


def exposure_rows(netted, collateral_rows):
    upper_rows = []
    lower_rows = []
    for index in range(len(collateral_rows)):
        net_gap = netted[:, index, :] - collateral_rows[index]
        upper_rows.append(jnp.sum(jnp.maximum(net_gap, 0.0), axis=0))
        lower_rows.append(jnp.sum(jnp.maximum(-net_gap, 0.0), axis=0))
    return (jnp.stack(upper_rows, axis=0), jnp.stack(lower_rows, axis=0))


def local(values, trade_set, lag_dates, threshold_cents, cap_cents):
    path_rows, date_rows, trades = values.shape
    set_count = lag_dates.shape[0]
    rim_depth = LAG_MAX + 1
    netting_book = membership(trade_set, set_count)
    netted = jnp.dot(
        values.reshape(-1, trades), netting_book, preferred_element_type=jnp.float32
    ).reshape(path_rows, date_rows, set_count)
    lower_bound = -threshold_cents.astype(jnp.float32) / 100.0
    upper_bound = cap_cents.astype(jnp.float32) / 100.0
    total_paths = path_rows * lax.axis_size("path")
    rim_rows = passed_along(
        netted[:, date_rows - rim_depth :, :].astype(jnp.bfloat16), "tm", 1
    ).astype(jnp.float32)
    date_list = [rim_rows[:, index, :] for index in range(rim_depth)]
    date_list = date_list + [netted[:, index, :] for index in range(date_rows)]
    margin_moves = moves_list(date_list, lag_dates, date_rows)
    full_shape = (path_rows, set_count)
    lower_rows = jnp.broadcast_to(lower_bound, full_shape)
    upper_rows = jnp.broadcast_to(upper_bound, full_shape)
    state = (margin_moves[0], lower_rows, upper_rows)
    prefix_list = [state]
    for index in range(1, date_rows):
        state = compose(state, (margin_moves[index], lower_rows, upper_rows))
        prefix_list.append(state)
    neutral = (
        jnp.zeros(full_shape, jnp.float32),
        jnp.full(full_shape, -1e30, jnp.float32),
        jnp.full(full_shape, 1e30, jnp.float32),
    )
    incoming = entering(state, "tm", compose, neutral)
    start_balance = jnp.minimum(jnp.maximum(incoming[0], incoming[1]), incoming[2])
    collateral_rows = [
        jnp.minimum(jnp.maximum(start_balance + item[0], item[1]), item[2]) for item in prefix_list
    ]
    epe_part, ene_part = exposure_rows(netted, collateral_rows)
    epe_sum, ene_sum = lax.psum((epe_part, ene_part), "path")
    return (epe_sum / total_paths, ene_sum / total_paths)


def solution(mesh):
    placed = (P("path", "tm", None), P(), P(), P(), P())
    return jax.shard_map(
        local, mesh=mesh, in_specs=placed, out_specs=(P("tm", None), P("tm", None)), check_vma=False
    )
```

profile of v0, /device:TPU:0, one launch (start us, length us, event | category | flops | bytes accessed | tf_op | source)
XLA Modules:
  0.0 148.1 jit_solution(1931352760841294173)
XLA Ops:
  7.2 13.4 %fusion.3 = f32[1024,512]{0,1:T(8,128)S(1)} fusion(bf16[512,8192]{1,0:T(8,128)(2,1)} %bitcast.1597, s32[8192]{0:T(1024)} %param.8), kind=kOutput, calls=%fused_computation.11 | convolution fusion | flops 8598323200 | bytes 10518528 | tf_op jit(solution)/shard_map/dot_general | solution.py:74
  20.7 0.8 copy.449
  21.5 3.0 %collective-permute-start = (bf16[16,5,1024]{2,0,1:T(8,128)(2,1)}, bf16[16,5,1024]{2,0,1:T(8,128)(2,1)}, u32[]{:S(2)}, u32[]{:S(2)}) collective-permute-start(bf16[16,5,1024]{2,0,1:T(8,128)(2,1)} %copy.449), channel_id=1, source_target_pairs={{0,1},{1,2},{2,3},{4,5},{5,6},{6,7},{8,9},{9,10},{10,11},{12,13},{... | collective-permute-start | bytes 491528 | tf_op jit(solution)/shard_map/ppermute | solution.py:12
  24.5 1.4 fusion.269
  25.9 1.8 %fusion.268 = (f32[16,1,1024]{2,1,0:T(1,128)}, f32[16,1,1024]{2,1,0:T(1,128)S(1)}, f32[16,1,1024]{2,1,0:T(1,128)S(1)}, f32[16,1,1024]{2,1,0:T(1,128)S(1)}, f32[1...) fusion(f32[16,32,1024]{2,1,0:T(8,128)S(1)} %bitcast.1532), kind=kLoop, calls=%fused_computation.689 | loop fusion | bytes 2490368 | tf_op jit(solution)/shard_map/slice | solution.py:63
  27.8 1.9 %fusion.48 = (f32[16,1024]{1,0:T(8,128)}, f32[16,1024]{1,0:T(8,128)}, f32[16,1024]{1,0:T(8,128)}, f32[16,1024]{1,0:T(8,128)}, f32[16,1024]{1,0:T(8,128)}, /*inde...) fusion(f32[16,1,1024]{2,1,0:T(1,128)} %get-tuple-element.377, ...), kind=kLoop, calls=%fused_computation.122 | loop fusion | flops 1261568 | bytes 1654784 | tf_op jit(solution)/shard_map/add | solution.py:54
  29.7 2.0 %fusion.84 = (f32[16,1024]{1,0:T(8,128)S(1)}, f32[16,1024]{1,0:T(8,128)S(1)}, f32[16,1024]{1,0:T(8,128)S(1)}, f32[16,1024]{1,0:T(8,128)S(1)}, f32[16,1024]{1,0:T...) fusion(f32[16,1,1024]{2,1,0:T(1,128)} %get-tuple-element.390, ...), kind=kLoop, calls=%fused_computation.218 | loop fusion | flops 1376256 | bytes 1785856 | tf_op jit(solution)/shard_map/add | solution.py:54
  31.7 0.7 convert_multiply_fusion
  32.3 0.9 convert_element_type.84
  33.3 1.7 %fusion.96 = (f32[16,1024]{1,0:T(8,128)}, f32[16,1024]{1,0:T(8,128)}, f32[16,1024]{1,0:T(8,128)}, f32[16,1024]{1,0:T(8,128)}, f32[16,1024]{1,0:T(8,128)}, /*index=5*/f32[16,1024]{1,0:T(8,128)}) fusion(f32[16,5,1024]{2,0,1:T(8,128)S(1)} %convert_element_type.84, f32[16,1,1024]{2,1,0:T(1,128)} %get-tuple-element.382, f32[16,1,1024]{2,1,0:T(1,128)} %get-tuple-element.363, ...), kind=kLoop, calls=%fused_computation.250 | loop fusion | flops 688128 | bytes 999424 | tf_op jit(solution)/shard_map/add | solution.py:54
  35.0 2.3 %minimum_convert_fusion = (bf16[1,16,1024]{2,1,0:T(8,128)(2,1)S(1)}, f32[1,16,1024]{2,1,0:T(8,128)S(1)}, f32[1,16,1024]{2,1,0:T(8,128)S(1)}, f32[1,16,1024]{2,1,...) fusion(f32[1024]{0:T(1024)S(1)} %convert_multiply_fusion, ...), kind=kLoop, calls=%fused_computation.663 | loop fusion | flops 5718016 | bytes 4448256 | tf_op jit(solution)/shard_map/convert_element_type | solution.py:18
  37.3 0.2 add_convert_fusion
  37.6 0.4 minimum_convert_fusion.1
  38.0 6.2 %all_gather.13 = bf16[4,16,1024]{2,1,0:T(8,128)(2,1)S(1)} all-gather(bf16[1,16,1024]{2,1,0:T(8,128)(2,1)S(1)} %minimum_convert_fusion.1), channel_id=1, replica_groups=mesh['path'=8,'tm'=4] {'tm'}, dimensions={0}, use_global_device_ids=true | all-gather | bytes 163840 | tf_op jit(solution)/shard_map/all_gather | solution.py:18
  44.2 5.4 %all_gather.12 = bf16[4,16,1024]{2,1,0:T(8,128)(2,1)S(1)} all-gather(bf16[1,16,1024]{2,1,0:T(8,128)(2,1)S(1)} %add_convert_fusion), channel_id=1, replica_groups=mesh['path'=8,'tm'=4] {'tm'}, dimensions={0}, use_global_device_ids=true | all-gather | bytes 163840 | tf_op jit(solution)/shard_map/all_gather | solution.py:18
  49.6 5.4 %all_gather.14 = bf16[4,16,1024]{2,1,0:T(8,128)(2,1)S(1)} all-gather(bf16[1,16,1024]{2,1,0:T(8,128)(2,1)S(1)} %get-tuple-element.327), channel_id=1, replica_groups=mesh['path'=8,'tm'=4] {'tm'}, dimensions={0}, use_global_device_ids=true | all-gather | bytes 163840 | tf_op jit(solution)/shard_map/all_gather | solution.py:18
  55.0 0.3 while.18
  55.4 2.6 %fusion.5 = (f32[16,1024]{1,0:T(8,128)S(1)}, f32[16,1024]{1,0:T(8,128)S(1)}, f32[16,1024]{1,0:T(8,128)S(1)}, f32[16,1024]{1,0:T(8,128)S(1)}, f32[16,1024]{1,0:T(...) fusion(f32[16,1,1024]{2,1,0:T(1,128)} %get-tuple-element.394, ...), kind=kLoop, calls=%fused_computation.15 | loop fusion | flops 4636672 | bytes 7561216 | tf_op jit(solution)/shard_map/sub | solution.py:63
  58.1 0.2 bitcast_subtract_fusion.5
  60.2 2.7 %stack.263 = f32[32,1024]{1,0:T(8,128)} concatenate(f32[1,1024]{1,0:T(1,128)S(1)} %bitcast.1596, f32[1,1024]{1,0:T(1,128)S(1)} %bitcast.1595, f32[1,1024]{1,0:T(1,128)S(1)} %bitcast.1552, f32[1,1024]{1,0:T(1,128)S(1)} %bitcast.1551, f32[1,1024]{1,0:T(1,128)S(1)} %bitcast.1556, f32[1,1024]{1,0:T(1,128)S(1)} %bitcast.1555, f32[1,1024]{1,0:T(1,128)S(1)} %bitcast.1594, ...), dimensions={0} | concatenate | bytes 262144 | tf_op jit(solution)/shard_map/stack | solution.py:66
  62.8 2.7 %stack.230 = f32[32,1024]{1,0:T(8,128)} concatenate(f32[1,1024]{1,0:T(1,128)S(1)} %bitcast.1580, f32[1,1024]{1,0:T(1,128)S(1)} %bitcast.1579, f32[1,1024]{1,0:T(1,128)S(1)} %bitcast.1541, f32[1,1024]{1,0:T(1,128)S(1)} %bitcast.1540, f32[1,1024]{1,0:T(1,128)S(1)} %bitcast.1545, f32[1,1024]{1,0:T(1,128)S(1)} %bitcast.1544, f32[1,1024]{1,0:T(1,128)S(1)} %bitcast.1578, ...), dimensions={0} | concatenate | bytes 262144 | tf_op jit(solution)/shard_map/stack | solution.py:66
  65.5 72.5 %all-reduce.3.cloned.1.call-done = (f32[32,1024]{1,0:T(8,128)}, f32[32,1024]{1,0:T(8,128)}) async-done(((f32[32,1024]{1,0:T(8,128)}, f32[32,1024]{1,0:T(8,128)}), (f32[32,1024]{1,0:T(8,128)}, f32[32,1024]{1,0:T(8,128)})) %all-reduce.3.cloned.1.call-update) | async-done | bytes 262160 | tf_op jit(solution)/shard_map/psum | solution.py:105
  138.1 1.6 %broadcast_multiply_fusion.1 = f32[32,1024]{1,0:T(8,128)} fusion(f32[32,1024]{1,0:T(8,128)} %get-tuple-element.253), kind=kLoop, calls=%fused_computation.569 | loop fusion | flops 32768 | bytes 262144 | tf_op jit(solution)/shard_map/div | solution.py:106
  139.6 1.6 %broadcast_multiply_fusion = f32[32,1024]{1,0:T(8,128)} fusion(f32[32,1024]{1,0:T(8,128)} %get-tuple-element.254), kind=kLoop, calls=%fused_computation.568 | loop fusion | flops 32768 | bytes 262144 | tf_op jit(solution)/shard_map/div | solution.py:106
  (74 shorter events, 2.1 us)
Async XLA Ops:
  7.2 130.9 %all-reduce.3.cloned.1.call-start = ((), (), s32[]{:S(2)}) async-start(), calls=%async_computation | async-start | bytes 524288 | tf_op jit(solution)/shard_map/psum | solution.py:105
  7.2 20.5 %copy-start.17 = (s32[1024]{0:T(1024)S(1)}, s32[1024]{0:T(1024)}, u32[]{:S(2)}) copy-start(s32[1024]{0:T(1024)} %param.10) | copy-start | bytes 12292
  7.2 20.5 %copy-start.16 = (s32[1024]{0:T(1024)S(1)}, s32[1024]{0:T(1024)}, u32[]{:S(2)}) copy-start(s32[1024]{0:T(1024)} %param.9) | copy-start | bytes 12292
  21.5 10.9 %collective-permute-start = (bf16[16,5,1024]{2,0,1:T(8,128)(2,1)}, bf16[16,5,1024]{2,0,1:T(8,128)(2,1)}, u32[]{:S(2)}, u32[]{:S(2)}) collective-permute-start(bf16[16,5,1024]{2,0,1:T(8,128)(2,1)} %copy.449), channel_id=1, source_target_pairs={{0,1},{1,2},{2,3},{4,5},{5,6},{6,7},{8,9},{9,10},{10,11},{12,13},{... | collective-permute-start | bytes 491528 | tf_op jit(solution)/shard_map/ppermute | solution.py:12
  27.7 9.6 %copy-start.12 = (f32[1024]{0:T(1024)}, f32[1024]{0:T(1024)S(1)}, u32[]{:S(2)}) copy-start(f32[1024]{0:T(1024)S(1)} %get-tuple-element.469) | copy-start | bytes 12292
  27.7 9.6 %copy-start.14 = (f32[1024]{0:T(1024)}, f32[1024]{0:T(1024)S(1)}, u32[]{:S(2)}) copy-start(f32[1024]{0:T(1024)S(1)} %get-tuple-element.470) | copy-start | bytes 12292
  37.3 20.8 %copy-start.10 = (f32[16,1,1024]{2,1,0:T(1,128)S(1)}, f32[16,1,1024]{2,1,0:T(1,128)}, u32[]{:S(2)}) copy-start(f32[16,1,1024]{2,1,0:T(1,128)} %get-tuple-element.370) | copy-start | bytes 196612
  37.5 21.0 %copy-start.9 = (f32[16,1,1024]{2,1,0:T(1,128)S(1)}, f32[16,1,1024]{2,1,0:T(1,128)}, u32[]{:S(2)}) copy-start(f32[16,1,1024]{2,1,0:T(1,128)} %get-tuple-element.363) | copy-start | bytes 196612
  37.6 21.0 %copy-start.11 = (f32[16,1,1024]{2,1,0:T(1,128)S(1)}, f32[16,1,1024]{2,1,0:T(1,128)}, u32[]{:S(2)}) copy-start(f32[16,1,1024]{2,1,0:T(1,128)} %get-tuple-element.382) | copy-start | bytes 196612
  37.6 21.2 %copy-start.6 = (f32[16,1,1024]{2,1,0:T(1,128)S(1)}, f32[16,1,1024]{2,1,0:T(1,128)}, u32[]{:S(2)}) copy-start(f32[16,1,1024]{2,1,0:T(1,128)} %get-tuple-element.388) | copy-start | bytes 196612
  37.6 21.2 %copy-start.7 = (f32[16,1,1024]{2,1,0:T(1,128)S(1)}, f32[16,1,1024]{2,1,0:T(1,128)}, u32[]{:S(2)}) copy-start(f32[16,1,1024]{2,1,0:T(1,128)} %get-tuple-element.389) | copy-start | bytes 196612
  37.6 21.2 %copy-start.8 = (f32[16,1,1024]{2,1,0:T(1,128)S(1)}, f32[16,1,1024]{2,1,0:T(1,128)}, u32[]{:S(2)}) copy-start(f32[16,1,1024]{2,1,0:T(1,128)} %get-tuple-element.390) | copy-start | bytes 196612
  38.0 21.0 %copy-start.2 = (f32[16,1,1024]{2,1,0:T(1,128)S(1)}, f32[16,1,1024]{2,1,0:T(1,128)}, u32[]{:S(2)}) copy-start(f32[16,1,1024]{2,1,0:T(1,128)} %get-tuple-element.384) | copy-start | bytes 196612
  38.0 21.0 %copy-start.3 = (f32[16,1,1024]{2,1,0:T(1,128)S(1)}, f32[16,1,1024]{2,1,0:T(1,128)}, u32[]{:S(2)}) copy-start(f32[16,1,1024]{2,1,0:T(1,128)} %get-tuple-element.385) | copy-start | bytes 196612
  38.0 21.0 %copy-start.4 = (f32[16,1,1024]{2,1,0:T(1,128)S(1)}, f32[16,1,1024]{2,1,0:T(1,128)}, u32[]{:S(2)}) copy-start(f32[16,1,1024]{2,1,0:T(1,128)} %get-tuple-element.386) | copy-start | bytes 196612
  38.0 21.0 %copy-start.5 = (f32[16,1,1024]{2,1,0:T(1,128)S(1)}, f32[16,1,1024]{2,1,0:T(1,128)}, u32[]{:S(2)}) copy-start(f32[16,1,1024]{2,1,0:T(1,128)} %get-tuple-element.387) | copy-start | bytes 196612
  55.0 4.2 %copy-start.1 = (f32[16,1,1024]{2,1,0:T(1,128)S(1)}, f32[16,1,1024]{2,1,0:T(1,128)}, u32[]{:S(2)}) copy-start(f32[16,1,1024]{2,1,0:T(1,128)} %get-tuple-element.383) | copy-start | bytes 196612
  55.4 2.9 %copy-start.13 = (f32[1024]{0:T(1024)S(1)}, f32[1024]{0:T(1024)}, u32[]{:S(2)}) copy-start(f32[1024]{0:T(1024)} %copy-done.12) | copy-start | bytes 12292
  55.4 2.9 %copy-start.15 = (f32[1024]{0:T(1024)S(1)}, f32[1024]{0:T(1024)}, u32[]{:S(2)}) copy-start(f32[1024]{0:T(1024)} %copy-done.14) | copy-start | bytes 12292
  55.4 4.0 %copy-start = (f32[16,1,1024]{2,1,0:T(1,128)S(1)}, f32[16,1,1024]{2,1,0:T(1,128)}, u32[]{:S(2)}) copy-start(f32[16,1,1024]{2,1,0:T(1,128)} %get-tuple-element.377) | copy-start | bytes 196612
Sparse Core Ops, SparseCore 0:
  65.7 72.3 all-reduce.2
where the time goes:
time: 149 us; the launch traced here: 148 us
  waiting for transfers between devices  72.6 us (49%)
  other arithmetic  18 us (12%)
  blocking collectives  17 us (11%)
  between operations  14.5 us (10%)
  matrix products  13.4 us (9%)
  local copies, waits for them, and re-layouts  9.42 us (6%)
  starting transfers between devices  3.08 us (2%)
    psum x1, waiting for transfers between devices, local(): epe_sum, ene_sum = lax.psum((epe_part, ene_part), 'path')  72.5 us
    all_gather x3, blocking collectives, entering(): lax.all_gather(part.astype(kind), axis)  17 us
    dot_general x1, matrix products, local(): jnp.dot(values.reshape(-1, trades), netting_book, preferred_element_type=...  13.4 us
    add x3, other arithmetic, moves_list(): total = total + lag_masks[offset - 1] * date_list[LAG_MAX - offset + index]  5.61 us
    another operation x2, local copies, waits for them, and re-layouts, exposure_rows(): return (jnp.stack(upper_rows, axis=0), jnp.stack(lower_rows, axis=0))  5.33 us
    sub x9, other arithmetic, exposure_rows(): net_gap = netted[:, index, :] - collateral_rows[index]  3.62 us
    div x2, other arithmetic, local(): return (epe_sum / total_paths, ene_sum / total_paths)  3.14 us
    ppermute x1, starting transfers between devices, passed_along(): lax.ppermute(value, axis, [(source, source + steps) for source in range(f...  3.05 us
  transfers between devices with their start and end apart: 2, of which 1 were waited for; matrix products, arithmetic and copies ran while one was open for 5% of the time, Pallas kernels for 0%

commit v1 on v0

v1 whole, which is shorter than its diff:
```python
import functools

import jax
import jax.numpy as jnp
from jax import lax
from jax.experimental import pallas as pl
from jax.experimental.pallas import tpu as pltpu
from jax.sharding import PartitionSpec as P

LAG_MAX = 4
RIM = LAG_MAX + 1
LANES = 128
F32 = jnp.float32
BF16 = jnp.bfloat16
MESH = pl.DeviceIdType.MESH


def clip(x, low, high):
    return jnp.minimum(jnp.maximum(x, low), high)


def kernel(
    path_count, tm_count, paths, dates, width, depth,
    values_ref, trades_ref, lags_ref, bounds_ref, out_ref,
    held, netted, outbox, inbox, sums, parts, pieces, finals,
    load_sem, tm_send, tm_recv, rs_send, rs_recv, ag_send, ag_recv,
):
    rows, trades = values_ref.shape
    sets = lags_ref.shape[1]
    chunks = sets // width
    tiles = width // LANES
    steps = trades // depth
    piece_rows = parts.shape[2]
    here_path, here_tm = lax.axis_index("path"), lax.axis_index("tm")

    def load(step):
        columns = pl.ds(pl.multiple_of(step * depth, depth), depth)
        return pltpu.make_async_copy(values_ref.at[:, columns], held.at[:, columns], load_sem.at[step])

    for step in range(steps):
        load(step).start()

    def greet(j, carry):
        pl.semaphore_signal(
            barrier, inc=1, device_id={"path": lax.rem(here_path + j, path_count)}, device_id_type=MESH
        )
        return carry

    barrier = pltpu.get_barrier_semaphore()
    lax.fori_loop(1, path_count, greet, 0)
    for j in range(1, tm_count):
        pl.semaphore_signal(
            barrier, inc=1, device_id={"tm": lax.rem(here_tm + j, tm_count)}, device_id_type=MESH
        )

    for j in range(1, tm_count):
        @pl.when(here_tm < j)
        def _(j=j):
            inbox[:, j - 1] = jnp.zeros(inbox.shape[:1] + inbox.shape[2:], BF16)

    def tm_copy(c, j):
        first, count = (2, 3 + RIM) if j == 1 else (0, 4)
        return pltpu.make_async_remote_copy(
            src_ref=outbox.at[c, pl.ds(first, count)],
            dst_ref=inbox.at[c, j - 1, pl.ds(first, count)],
            send_sem=tm_send.at[c, j - 1],
            recv_sem=tm_recv.at[c, j - 1],
            device_id={"tm": lax.rem(here_tm + j, tm_count)},
            device_id_type=MESH,
        )

    def rs_copy(c, j):
        to = lax.rem(here_path + j, path_count)
        return pltpu.make_async_remote_copy(
            src_ref=parts.at[c, to],
            dst_ref=pieces.at[c, j - 1],
            send_sem=rs_send.at[c],
            recv_sem=rs_recv.at[c],
            device_id={"path": to},
            device_id_type=MESH,
        )

    def ag_copy(c, j):
        columns = pl.ds(c * width, width)
        return pltpu.make_async_remote_copy(
            src_ref=finals.at[c],
            dst_ref=out_ref.at[here_path, :, columns],
            send_sem=ag_send.at[c],
            recv_sem=ag_recv.at[c],
            device_id={"path": lax.rem(here_path + j, path_count)},
            device_id_type=MESH,
        )

    def start_all(copy, c):
        def one(j, carry):
            copy(c, j).start()
            return carry
        lax.fori_loop(1, path_count, one, 0)

    set_rows = lax.broadcasted_iota(jnp.int32, (width, depth), 0)

    def multiply(c):
        def step_of(step, carry):
            if c == 0:
                load(step).wait()
            columns = pl.ds(pl.multiple_of(step * depth, depth), depth)
            book = jnp.where(trades_ref[:, columns] - c * width == set_rows, 1.0, 0.0).astype(BF16)
            product = lax.dot_general(
                held[:, columns], book, (((1,), (1,)), ((), ())), preferred_element_type=F32
            )
            for k in range(tiles):
                part = product[:, k * LANES:(k + 1) * LANES]
                netted[c % 2, k] = jnp.where(step == 0, part, netted[c % 2, k] + part)
            return carry
        lax.fori_loop(0, steps, step_of, 0)

    def dated(c, k, t):
        return netted[c % 2, k, pl.ds(t, paths, stride=dates), :]

    def span(c, k):
        return pl.ds(c * width + k * LANES, LANES)

    def limits(c, k):
        shape = (paths, LANES)
        low = jnp.broadcast_to(bounds_ref[0:1, span(c, k)], shape)
        high = jnp.broadcast_to(bounds_ref[1:2, span(c, k)], shape)
        return low, high

    def lag_of(c, k):
        return jnp.broadcast_to(lags_ref[0:1, span(c, k)], (paths, LANES))

    def summarize(c):
        every = range(tiles)
        bounds = [limits(c, k) for k in every]
        lags = [lag_of(c, k) for k in every]

        def advance(t, state):
            new = []
            for k in every:
                before, low_edge, high_edge = state[k]
                now = dated(c, k, t)
                move = now - before
                low, high = bounds[k]
                new.append((now, clip(low_edge + move, low, high), clip(high_edge + move, low, high)))
            return tuple(new)

        state = tuple((dated(c, k, 1), *bounds[k]) for k in every)
        state = lax.fori_loop(2, dates - RIM + 1, advance, state, unroll=True)
        cut = [s[1:] for s in state]
        for t in range(dates - RIM + 1, dates):
            state = advance(t, state)
            for k in every:
                if t < dates - 1:
                    keep = lags[k] <= dates - 1 - t
                    cut[k] = tuple(jnp.where(keep, new, old) for new, old in zip(state[k][1:], cut[k]))
        for k in every:
            lanes = pl.ds(k * LANES, LANES)
            outbox[c, 0, :, lanes] = state[k][1].astype(BF16)
            outbox[c, 1, :, lanes] = state[k][2].astype(BF16)
            outbox[c, 2, :, lanes] = dated(c, k, 0).astype(BF16)
            for back in range(RIM):
                outbox[c, 3 + back, :, lanes] = dated(c, k, dates - 1 - back).astype(BF16)
            outbox[c, 3 + RIM, :, lanes] = cut[k][0].astype(BF16)
            outbox[c, 4 + RIM, :, lanes] = cut[k][1].astype(BF16)
        for j in range(1, tm_count):
            @pl.when(here_tm + j < tm_count)
            def _(j=j):
                tm_copy(c, j).start()

    def expose(c):
        every = range(tiles)
        for j in range(1, tm_count):
            @pl.when(here_tm >= j)
            def _(j=j):
                tm_copy(c, j).wait_recv()

        def picked(masks, window):
            out = window[3]
            for index in (2, 1, 0):
                out = jnp.where(masks[index], window[index], out)
            return out

        masks, state = [], []
        for k in every:
            lanes = pl.ds(k * LANES, LANES)
            low, high = limits(c, k)
            lag = lag_of(c, k)
            mask = [lag == offset for offset in range(1, LAG_MAX)]

            def got(j, index):
                return inbox[c, j - 1, index, :, lanes].astype(F32)

            balance = jnp.zeros((paths, LANES), F32)
            last = balance
            for j in range(tm_count - 1, 1, -1):
                first, end = got(j, 2), got(j, 3)
                balance = clip(balance + (first - last), low, high)
                balance = clip(balance + (end - first), got(j, 0), got(j, 1))
                last = end
            first = got(1, 2)
            rim = [got(1, 3 + back) for back in range(RIM)]
            lagged = picked(mask, rim[1:])
            balance = clip(balance + (first - last), low, high)
            balance = jnp.where(here_tm > 0, balance, 0.0)
            balance = clip(balance + (lagged - first), got(1, 3 + RIM), got(1, 4 + RIM))
            masks.append(mask)
            state.append((balance, lagged, *rim[:LAG_MAX]))
        bounds = [limits(c, k) for k in every]

        def advance(t, state):
            new = []
            for k in every:
                balance, before, *window = state[k]
                low, high = bounds[k]
                now = dated(c, k, t)
                lagged = picked(masks[k], window)
                balance = clip(balance + (lagged - before), low, high)
                gap = now - balance
                above = jnp.maximum(gap, 0.0)
                below = above - gap
                for side, amount in enumerate((above, below)):
                    folded = amount[0:8]
                    for at in range(8, paths, 8):
                        folded = folded + amount[at:at + 8]
                    sums[k, pl.ds(pl.multiple_of((side * dates + t) * 8, 8), 8), :] = folded
                new.append((balance, lagged, now, *window[:LAG_MAX - 1]))
            return tuple(new)

        lax.fori_loop(0, dates, advance, tuple(state), unroll=True)
        for k in every:
            total = sums[k, pl.ds(0, 2 * dates, stride=8), :]
            for at in range(1, 8):
                total = total + sums[k, pl.ds(at, 2 * dates, stride=8), :]
            total = total.reshape(path_count, piece_rows, LANES)
            parts[c, :, :, pl.ds(k * LANES, LANES)] = total.astype(BF16)
        start_all(rs_copy, c)

    def arrived(ref, sem):
        return pltpu.make_async_copy(ref, ref, sem)

    def finish(c):
        box = pieces.at[c]
        arrived(box, rs_recv.at[c]).wait()
        total = parts[c, here_path].astype(F32)
        for j in range(path_count - 1):
            total = total + pieces[c, j].astype(F32)
        total = total * (1.0 / (paths * path_count))
        finals[c] = total
        out_ref[here_path, :, pl.ds(c * width, width)] = total
        start_all(ag_copy, c)

    for c in range(chunks):
        multiply(c)
        if c == 0:
            pl.semaphore_wait(barrier, path_count + tm_count - 2)
        summarize(c)
        if c >= 1:
            expose(c - 1)
        if c >= 2:
            finish(c - 2)
    expose(chunks - 1)
    for c in range(max(0, chunks - 2), chunks):
        finish(c)
    for c in range(chunks):
        for j in range(1, tm_count):
            @pl.when(here_tm + j < tm_count)
            def _(j=j):
                tm_copy(c, j).wait_send()
        arrived(pieces.at[c], rs_send.at[c]).wait()
        box = out_ref.at[pl.ds(0, path_count - 1), :, pl.ds(c * width, width)]
        arrived(box, ag_send.at[c]).wait()
        arrived(box, ag_recv.at[c]).wait()


def solution(mesh):
    path_count, tm_count = mesh.shape["path"], mesh.shape["tm"]

    def local(values, trade_set, lag_dates, threshold_cents, cap_cents):
        paths, dates, trades = values.shape
        sets = lag_dates.shape[0]
        width = 2 * LANES
        depth = 1024
        chunks, steps, tiles = sets // width, trades // depth, width // LANES
        piece_rows = 2 * dates // path_count
        rows = paths * dates
        bounds = jnp.stack(
            [-threshold_cents.astype(F32) / 100.0, cap_cents.astype(F32) / 100.0]
        )
        dma = pltpu.SemaphoreType.DMA
        out = pl.pallas_call(
            functools.partial(kernel, path_count, tm_count, paths, dates, width, depth),
            out_shape=jax.ShapeDtypeStruct((path_count, piece_rows, sets), F32),
            in_specs=[pl.BlockSpec(memory_space=pl.ANY)] + [pl.BlockSpec(memory_space=pltpu.VMEM)] * 3,
            out_specs=pl.BlockSpec(memory_space=pltpu.VMEM),
            scratch_shapes=[
                pltpu.VMEM((rows, trades), BF16),
                pltpu.VMEM((2, tiles, rows, LANES), F32),
                pltpu.VMEM((chunks, 5 + RIM, paths, width), BF16),
                pltpu.VMEM((chunks, tm_count - 1, 5 + RIM, paths, width), BF16),
                pltpu.VMEM((tiles, 2 * dates * 8, LANES), F32),
                pltpu.VMEM((chunks, path_count, piece_rows, width), BF16),
                pltpu.VMEM((chunks, path_count - 1, piece_rows, width), BF16),
                pltpu.VMEM((chunks, piece_rows, width), F32),
                dma((steps,)),
                dma((chunks, tm_count - 1)),
                dma((chunks, tm_count - 1)),
                dma((chunks,)),
                dma((chunks,)),
                dma((chunks,)),
                dma((chunks,)),
            ],
            compiler_params=pltpu.CompilerParams(
                collective_id=0, has_side_effects=True, vmem_limit_bytes=48 * 2**20
            ),
        )(values.reshape(rows, trades), trade_set[None, :], lag_dates[None, :], bounds)
        out = out.reshape(2 * dates, sets)
        return out[:dates], out[dates:]

    placed = (P("path", "tm", None), P(), P(), P(), P())
    return jax.shard_map(
        local, mesh=mesh, in_specs=placed, out_specs=(P("tm", None), P("tm", None)), check_vma=False
    )
```

time: 149 us -> 36.5 us (0.24)
  waiting for transfers between devices: 72.6 us -> 0 us
  Pallas kernels: 0 us -> 32 us
  blocking collectives: 17 us -> 0 us
  other arithmetic: 18 us -> 1.39 us
  between operations: 14.5 us -> 0.65 us
  matrix products: 13.4 us -> 0 us
  local copies, waits for them, and re-layouts: 9.42 us -> 2.16 us
  starting transfers between devices: 3.08 us -> 0 us
    psum x1 -> x0, waiting for transfers between devices: 72.5 us -> none  [local(): epe_sum, ene_sum = lax.psum((epe_part, ene_part), 'path')]
    pallas_call x0 -> x1, Pallas kernels: none -> 32 us  [local(): pl.pallas_call(functools.partial(kernel, path_count, tm_count, paths, dat...]
    all_gather x3 -> x0, blocking collectives: 17 us -> none  [entering(): lax.all_gather(part.astype(kind), axis)]
    dot_general x1 -> x0, matrix products: 13.4 us -> none  [local(): jnp.dot(values.reshape(-1, trades), netting_book, preferred_element_type=...]
    add x3 -> x0, other arithmetic: 5.61 us -> none  [moves_list(): total = total + lag_masks[offset - 1] * date_list[LAG_MAX - offset + index]]
    another operation x2 -> x0, local copies, waits for them, and re-layouts: 5.33 us -> none  [exposure_rows(): return (jnp.stack(upper_rows, axis=0), jnp.stack(lower_rows, axis=0))]
    convert_element_type x5 -> x0, other arithmetic: 3.83 us -> none  [the longest x3 2.89 us: entering(): part.astype(kind)]
    sub x9 -> x0, other arithmetic: 3.62 us -> none  [exposure_rows(): net_gap = netted[:, index, :] - collateral_rows[index]]
  transfers between devices with their start and end apart: 2 -> 0, of which waited for: 1 -> 0; matrix products, arithmetic and copies ran while one was open for 5% -> 0% of each run, Pallas kernels for 0% -> 0%
where the time goes in v1:
time: 36.5 us; the launch traced here: 36.2 us
  Pallas kernels  32 us (88%)
  local copies, waits for them, and re-layouts  2.16 us (6%)
  other arithmetic  1.39 us (4%)
  between operations  0.65 us (2%)
    pallas_call x1, Pallas kernels, local(): pl.pallas_call(functools.partial(kernel, path_count, tm_count, paths, dat...  32 us
    unnamed x4, local copies, waits for them, and re-layouts  1.44 us

profile of v1, /device:TPU:0, one launch (start us, length us, event | category | flops | bytes accessed | tf_op | source)
XLA Modules:
  0.0 36.2 jit_solution(18278857018771872242)
XLA Ops:
  0.6 0.7 %negate_multiply_fusion = f32[1024]{0:T(1024)S(1)} fusion(s32[1024]{0:T(1024)} %param.8), kind=kLoop, calls=%fused_computation.4 | loop fusion | flops 3072 | bytes 8192 | tf_op jit(solution)/shard_map/div | solution.py:287
  1.3 0.7 %convert_multiply_fusion = f32[1024]{0:T(1024)S(1)} fusion(s32[1024]{0:T(1024)} %param.9), kind=kLoop, calls=%fused_computation.3 | loop fusion | flops 2048 | bytes 8192 | tf_op jit(solution)/shard_map/div | solution.py:287
  2.0 0.0 copy-start
  2.0 0.7 %copy-done = s32[8192]{0:T(1024)S(1)} copy-done((s32[8192]{0:T(1024)S(1)}, s32[8192]{0:T(1024)}, u32[]{:S(2)}) %copy-start) | copy-done | bytes 32792
  2.8 0.0 copy-start.1
  2.8 0.7 %copy-done.1 = s32[1024]{0:T(1024)S(1)} copy-done((s32[1024]{0:T(1024)S(1)}, s32[1024]{0:T(1024)}, u32[]{:S(2)}) %copy-start.1) | copy-done | bytes 4120
  3.5 32.0 %shard_map.68 = f32[8,8,1024]{2,1,0:T(8,128)S(1)} custom-call(bf16[512,8192]{1,0:T(8,128)(2,1)} %bitcast.11, s32[1,8192]{1,0:T(1,128)S(1)} %bitcast.9, s32[1,1024]{1,0:T(1,128)S(1)} %bitcast.10, f32[2,1024]{1,0:T(2,128)S(1)} %pad_maximum_fusion.bounds_ref), custom_call_target="tpu_custom_call" | custom-call | tf_op jit(solution)/shard_map/pallas_call | solution.py:290
  35.5 0.7 %slice_bitcast_fusion = (f32[32,1024]{1,0:T(8,128)}, f32[32,1024]{1,0:T(8,128)}) fusion(f32[8,8,1024]{2,1,0:T(8,128)S(1)} %shard_map.68), kind=kLoop, calls=%fused_computation | loop fusion | bytes 524288 | tf_op jit(solution)/shard_map/slice | solution.py:317
  (1 shorter events, 0.0 us)
Async XLA Ops:
  2.0 0.8 %copy-start = (s32[8192]{0:T(1024)S(1)}, s32[8192]{0:T(1024)}, u32[]{:S(2)}) copy-start(s32[8192]{0:T(1024)} %param.6) | copy-start | bytes 98308
  2.8 0.7 %copy-start.1 = (s32[1024]{0:T(1024)S(1)}, s32[1024]{0:T(1024)}, u32[]{:S(2)}) copy-start(s32[1024]{0:T(1024)} %param.7) | copy-start | bytes 12292

commit v2 on v1

v2 whole, which is shorter than its diff:
```python
import functools

import jax
import jax.numpy as jnp
from jax import lax
from jax.experimental import pallas as pl
from jax.experimental.pallas import tpu as pltpu
from jax.sharding import PartitionSpec as P

LAG_MAX = 4
RIM = LAG_MAX + 1
LANES = 128
GROUP = 2 * LANES
F32 = jnp.float32
BF16 = jnp.bfloat16
MESH = pl.DeviceIdType.MESH


def clip(x, low, high):
    return jnp.minimum(jnp.maximum(x, low), high)


def kernel(
    path_count, tm_count, paths, dates, blocks, depths, owners,
    values_ref, trades_hbm, lags_hbm, thresholds_hbm, caps_hbm, out_ref,
    held, trades_ref, lags_ref, thresholds_ref, caps_ref,
    netted, outbox, inbox, sums, parts, pieces, finals,
    load_sem, small_sem, tm_send, tm_recv, rs_send, rs_recv, ag_send, ag_recv,
):
    rows, trades = values_ref.shape
    tiles = GROUP // LANES
    groups = lags_ref.shape[1] // GROUP
    depth = depths[0]
    piece_rows = parts.shape[1]
    base = (path_count - owners) // 2
    here_path, here_tm = lax.axis_index("path"), lax.axis_index("tm")
    place = here_path - base
    owns = jnp.logical_and(place >= 0, place < owners)

    small = [
        pltpu.make_async_copy(src, dst, small_sem.at[at])
        for at, (src, dst) in enumerate(
            ((trades_hbm, trades_ref), (lags_hbm, lags_ref), (thresholds_hbm, thresholds_ref), (caps_hbm, caps_ref))
        )
    ]

    def load(step):
        columns = pl.ds(pl.multiple_of(step * depth, depth), depth)
        return pltpu.make_async_copy(values_ref.at[:, columns], held.at[:, columns], load_sem.at[step])

    small[0].start()
    for step in range(trades // depth):
        load(step).start()
    for copy in small[1:]:
        copy.start()

    def greet(j, carry):
        pl.semaphore_signal(
            barrier, inc=1, device_id={"path": lax.rem(here_path + j, path_count)}, device_id_type=MESH
        )
        return carry

    barrier = pltpu.get_barrier_semaphore()
    lax.fori_loop(1, path_count, greet, 0)
    for j in range(1, tm_count):
        pl.semaphore_signal(
            barrier, inc=1, device_id={"tm": lax.rem(here_tm + j, tm_count)}, device_id_type=MESH
        )

    for j in range(1, tm_count):
        @pl.when(here_tm < j)
        def _(j=j):
            inbox[j - 1] = jnp.zeros(inbox.shape[1:], BF16)

    def lanes_of(g):
        return pl.ds(g * GROUP, GROUP)

    def tm_copy(g, j):
        first, count = (2, 3 + RIM) if j == 1 else (0, 4)
        return pltpu.make_async_remote_copy(
            src_ref=outbox.at[pl.ds(first, count), :, lanes_of(g)],
            dst_ref=inbox.at[j - 1, pl.ds(first, count), :, lanes_of(g)],
            send_sem=tm_send.at[g, j - 1],
            recv_sem=tm_recv.at[g, j - 1],
            device_id={"tm": lax.rem(here_tm + j, tm_count)},
            device_id_type=MESH,
        )

    def rs_start(g):
        def one(at, carry):
            to = base + at
            j = lax.rem(to - here_path + path_count, path_count)

            @pl.when(j > 0)
            def _():
                pltpu.make_async_remote_copy(
                    src_ref=parts.at[at, :, lanes_of(g)],
                    dst_ref=pieces.at[j - 1, :, lanes_of(g)],
                    send_sem=rs_send.at[g],
                    recv_sem=rs_recv.at[g],
                    device_id={"path": to},
                    device_id_type=MESH,
                ).start()
            return carry
        lax.fori_loop(0, owners, one, 0)

    def ag_start(g):
        def one(j, carry):
            pltpu.make_async_remote_copy(
                src_ref=finals.at[:, lanes_of(g)],
                dst_ref=out_ref.at[place, :, lanes_of(g)],
                send_sem=ag_send.at[g],
                recv_sem=ag_recv.at[g],
                device_id={"path": lax.rem(here_path + j, path_count)},
                device_id_type=MESH,
            ).start()
            return carry
        lax.fori_loop(1, path_count, one, 0)

    def multiply(b):
        begin, width = blocks[b]
        deep = depths[min(b, 1)]
        set_rows = lax.broadcasted_iota(jnp.int32, (width, deep), 0) + begin

        def step_of(step, carry):
            if b == 0:
                load(step).wait()
            columns = pl.ds(pl.multiple_of(step * deep, deep), deep)
            book = jnp.where(trades_ref[:, columns] == set_rows, 1.0, 0.0).astype(BF16)
            product = lax.dot_general(
                held[:, columns], book, (((1,), (1,)), ((), ())), preferred_element_type=F32
            )
            for k in range(width // LANES):
                part = product[:, k * LANES:(k + 1) * LANES]
                if trades // deep == 1:
                    netted[b % 2, k] = part
                else:
                    netted[b % 2, k] = jnp.where(step == 0, part, netted[b % 2, k] + part)
            return carry

        if trades // deep == 1:
            step_of(0, 0)
        else:
            lax.fori_loop(0, trades // deep, step_of, 0)

    def block_of(g):
        return next(b for b, (begin, width) in enumerate(blocks) if begin <= g * GROUP < begin + width)

    def dated(g, k, t):
        b = block_of(g)
        tile = (g * GROUP - blocks[b][0]) // LANES + k
        return netted[b % 2, tile, pl.ds(t, paths, stride=dates), :]

    def span(g, k):
        return pl.ds(g * GROUP + k * LANES, LANES)

    def limits(c, k):
        shape = (paths, LANES)
        low = jnp.broadcast_to(-thresholds_ref[:, span(c, k)].astype(F32) / 100.0, shape)
        high = jnp.broadcast_to(caps_ref[:, span(c, k)].astype(F32) / 100.0, shape)
        return low, high

    def lag_of(c, k):
        return jnp.broadcast_to(lags_ref[0:1, span(c, k)], (paths, LANES))

    def summarize(c):
        every = range(tiles)
        bounds = [limits(c, k) for k in every]
        lags = [lag_of(c, k) for k in every]

        def advance(t, state):
            new = []
            for k in every:
                before, low_edge, high_edge = state[k]
                now = dated(c, k, t)
                move = now - before
                low, high = bounds[k]
                new.append((now, clip(low_edge + move, low, high), clip(high_edge + move, low, high)))
            return tuple(new)

        state = tuple((dated(c, k, 1), *bounds[k]) for k in every)
        state = lax.fori_loop(2, dates - RIM + 1, advance, state, unroll=True)
        cut = [s[1:] for s in state]
        for t in range(dates - RIM + 1, dates):
            state = advance(t, state)
            for k in every:
                if t < dates - 1:
                    keep = lags[k] <= dates - 1 - t
                    cut[k] = tuple(jnp.where(keep, new, old) for new, old in zip(state[k][1:], cut[k]))
        for k in every:
            lanes = span(c, k)
            outbox[0, :, lanes] = state[k][1].astype(BF16)
            outbox[1, :, lanes] = state[k][2].astype(BF16)
            outbox[2, :, lanes] = dated(c, k, 0).astype(BF16)
            for back in range(RIM):
                outbox[3 + back, :, lanes] = dated(c, k, dates - 1 - back).astype(BF16)
            outbox[3 + RIM, :, lanes] = cut[k][0].astype(BF16)
            outbox[4 + RIM, :, lanes] = cut[k][1].astype(BF16)
        for j in range(1, tm_count):
            @pl.when(here_tm + j < tm_count)
            def _(j=j):
                tm_copy(c, j).start()

    def expose(c):
        every = range(tiles)
        for j in range(1, tm_count):
            @pl.when(here_tm >= j)
            def _(j=j):
                tm_copy(c, j).wait_recv()

        def picked(masks, window):
            out = window[3]
            for index in (2, 1, 0):
                out = jnp.where(masks[index], window[index], out)
            return out

        masks, state = [], []
        for k in every:
            lanes = span(c, k)
            low, high = limits(c, k)
            lag = lag_of(c, k)
            mask = [lag == offset for offset in range(1, LAG_MAX)]

            def got(j, index):
                return inbox[j - 1, index, :, lanes].astype(F32)

            balance = jnp.zeros((paths, LANES), F32)
            last = balance
            for j in range(tm_count - 1, 1, -1):
                first, end = got(j, 2), got(j, 3)
                balance = clip(balance + (first - last), low, high)
                balance = clip(balance + (end - first), got(j, 0), got(j, 1))
                last = end
            first = got(1, 2)
            rim = [got(1, 3 + back) for back in range(RIM)]
            lagged = picked(mask, rim[1:])
            balance = clip(balance + (first - last), low, high)
            balance = jnp.where(here_tm > 0, balance, 0.0)
            balance = clip(balance + (lagged - first), got(1, 3 + RIM), got(1, 4 + RIM))
            masks.append(mask)
            state.append((balance, lagged, *rim[:LAG_MAX]))
        bounds = [limits(c, k) for k in every]

        def advance(t, state):
            new = []
            for k in every:
                balance, before, *window = state[k]
                low, high = bounds[k]
                now = dated(c, k, t)
                lagged = picked(masks[k], window)
                balance = clip(balance + (lagged - before), low, high)
                gap = now - balance
                above = jnp.maximum(gap, 0.0)
                below = above - gap
                for side, amount in enumerate((above, below)):
                    folded = amount[0:8]
                    for at in range(8, paths, 8):
                        folded = folded + amount[at:at + 8]
                    sums[k, pl.ds(pl.multiple_of((side * dates + t) * 8, 8), 8), :] = folded
                new.append((balance, lagged, now, *window[:LAG_MAX - 1]))
            return tuple(new)

        lax.fori_loop(0, dates, advance, tuple(state), unroll=True)
        for k in every:
            total = sums[k, pl.ds(0, 2 * dates, stride=8), :]
            for at in range(1, 8):
                total = total + sums[k, pl.ds(at, 2 * dates, stride=8), :]
            parts[:, :, span(c, k)] = total.reshape(owners, piece_rows, LANES).astype(BF16)
        rs_start(c)

    def arrived(ref, sem):
        return pltpu.make_async_copy(ref, ref, sem)

    def finish(g):
        lanes = lanes_of(g)

        @pl.when(owns)
        def _():
            arrived(pieces.at[:, :, lanes], rs_recv.at[g]).wait()
            total = parts[place, :, lanes].astype(F32)
            for j in range(path_count - 1):
                total = total + pieces[j, :, lanes].astype(F32)
            total = total * (1.0 / (paths * path_count))
            finals[:, lanes] = total
            out_ref[place, :, lanes] = total
            ag_start(g)

    summarized, exposed, finished = [], [], []
    for b, (begin, width) in enumerate(blocks):
        if b == 0:
            small[0].wait()
        multiply(b)
        if b == 0:
            for copy in small[1:]:
                copy.wait()
            pl.semaphore_wait(barrier, path_count + tm_count - 2)
        fresh = list(range(begin // GROUP, (begin + width) // GROUP))
        for g in fresh:
            summarize(g)
        ready = [g for g in summarized if g not in exposed]
        due = [g for g in exposed if g not in finished]
        summarized += fresh
        for g in ready:
            expose(g)
            exposed.append(g)
        for g in due:
            finish(g)
            finished.append(g)
    for g in range(groups):
        if g not in exposed:
            expose(g)
    for g in range(groups):
        if g not in finished:
            finish(g)
    for g in range(groups):
        lanes = lanes_of(g)
        for j in range(1, tm_count):
            @pl.when(here_tm + j < tm_count)
            def _(j=j):
                tm_copy(g, j).wait_send()

        @pl.when(owns)
        def _():
            arrived(pieces.at[:, :, lanes].at[pl.ds(0, owners - 1)], rs_send.at[g]).wait()
            arrived(out_ref.at[pl.ds(0, owners - 1), :, lanes], ag_recv.at[g]).wait()
            arrived(pieces.at[:, :, pl.ds(0, 2 * GROUP)], ag_send.at[g]).wait()

        @pl.when(jnp.logical_not(owns))
        def _():
            arrived(parts.at[:, :, lanes], rs_send.at[g]).wait()
            arrived(out_ref.at[:, :, lanes], ag_recv.at[g]).wait()


def solution(mesh):
    path_count, tm_count = mesh.shape["path"], mesh.shape["tm"]

    def local(values, trade_set, lag_dates, threshold_cents, cap_cents):
        paths, dates, trades = values.shape
        sets = lag_dates.shape[0]
        owners = max(1, path_count // 2)
        piece_rows = 2 * dates // owners
        rows, groups, tiles = paths * dates, sets // GROUP, GROUP // LANES
        head = max(1, groups // 2) * GROUP
        blocks = [(0, head)] + [(at, GROUP) for at in range(head, sets, GROUP)]
        depths = (trades // 4, trades // 2)
        dma = pltpu.SemaphoreType.DMA
        out = pl.pallas_call(
            functools.partial(kernel, path_count, tm_count, paths, dates, blocks, depths, owners),
            out_shape=jax.ShapeDtypeStruct((owners, piece_rows, sets), F32),
            in_specs=[pl.BlockSpec(memory_space=pltpu.HBM)] * 5,
            out_specs=pl.BlockSpec(memory_space=pltpu.VMEM),
            scratch_shapes=[
                pltpu.VMEM((rows, trades), BF16),
                pltpu.VMEM((1, trades), jnp.int32),
                pltpu.VMEM((1, sets), jnp.int32),
                pltpu.VMEM((1, sets), jnp.int32),
                pltpu.VMEM((1, sets), jnp.int32),
                pltpu.VMEM((2, head // LANES, rows, LANES), F32),
                pltpu.VMEM((5 + RIM, paths, sets), BF16),
                pltpu.VMEM((tm_count - 1, 5 + RIM, paths, sets), BF16),
                pltpu.VMEM((tiles, 2 * dates * 8, LANES), F32),
                pltpu.VMEM((owners, piece_rows, sets), BF16),
                pltpu.VMEM((path_count - 1, piece_rows, sets), BF16),
                pltpu.VMEM((piece_rows, sets), F32),
                dma((trades // depths[0],)),
                dma((4,)),
                dma((groups, tm_count - 1)),
                dma((groups, tm_count - 1)),
                dma((groups,)),
                dma((groups,)),
                dma((groups,)),
                dma((groups,)),
            ],
            compiler_params=pltpu.CompilerParams(
                collective_id=0, has_side_effects=True, vmem_limit_bytes=56 * 2**20
            ),
        )(
            values.reshape(rows, trades), trade_set[None, :], lag_dates[None, :],
            threshold_cents[None, :], cap_cents[None, :],
        )
        out = out.reshape(2 * dates, sets)
        return out[:dates], out[dates:]

    placed = (P("path", "tm", None), P(), P(), P(), P())
    return jax.shard_map(
        local, mesh=mesh, in_specs=placed, out_specs=(P("tm", None), P("tm", None)), check_vma=False
    )
```

time: 36.5 us -> 31.5 us (0.86)
  Pallas kernels: 32 us -> 29 us
  other arithmetic: 1.39 us -> 0 us
  local copies, waits for them, and re-layouts: 2.16 us -> 1.69 us
    pallas_call x1, Pallas kernels: 32 us -> 29 us  [local(): pl.pallas_call(functools.partial(kernel, path_count, tm_count, paths, dat...]
    unnamed x4 -> x0, local copies, waits for them, and re-layouts: 1.44 us -> none
    div x2 -> x0, other arithmetic: 1.38 us -> none  [the longest x1 0.69 us: local(): -threshold_cents.astype(F32) / 100.0]
    slice x1, local copies, waits for them, and re-layouts: 0.72 us -> 1.69 us  [local(): return (out[:dates], out[dates:])]
where the time goes in v2:
time: 31.5 us; the launch traced here: 31.3 us
  Pallas kernels  29 us (92%)
  local copies, waits for them, and re-layouts  1.69 us (5%)
  between operations  0.64 us (2%)
    pallas_call x1, Pallas kernels, local(): pl.pallas_call(functools.partial(kernel, path_count, tm_count, paths, dat...  29 us
    slice x1, local copies, waits for them, and re-layouts, local(): return (out[:dates], out[dates:])  1.69 us

profile of v2, /device:TPU:0, one launch (start us, length us, event | category | flops | bytes accessed | tf_op | source)
XLA Modules:
  0.0 31.3 jit_solution(14210261007851853276)
XLA Ops:
  0.6 29.0 %shard_map.68 = f32[4,16,1024]{2,1,0:T(8,128)} custom-call(bf16[512,8192]{1,0:T(8,128)(2,1)} %bitcast.7, s32[1,8192]{1,0:T(1,128)} %bitcast.10, s32[1,1024]{1,0:T(1,128)} %bitcast.11, s32[1,1024]{1,0:T(1,128)} %bitcast.12, s32[1,1024]{1,0:T(1,128)} %bitcast.13), custom_call_target="tpu_custom_call" | custom-call | tf_op jit(solution)/shard_map/pallas_call | solution.py:347
  29.6 1.7 %fusion = (f32[2,16,1024]{2,1,0:T(8,128)}, f32[2,16,1024]{2,1,0:T(8,128)}) fusion(f32[4,16,1024]{2,1,0:T(8,128)} %shard_map.68), kind=kLoop, calls=%fused_computation | loop fusion | bytes 524288 | tf_op jit(solution)/shard_map/slice | solution.py:382

commit v3 on v2

--- a/solution.py
+++ b/solution.py
@@ -265,7 +265,7 @@
             total = sums[k, pl.ds(0, 2 * dates, stride=8), :]
             for at in range(1, 8):
                 total = total + sums[k, pl.ds(at, 2 * dates, stride=8), :]
-            parts[:, :, span(c, k)] = total.reshape(owners, piece_rows, LANES).astype(BF16)
+            parts[:, :, span(c, k)] = total.reshape(owners, piece_rows, LANES)
         rs_start(c)
 
     def arrived(ref, sem):
@@ -277,9 +277,9 @@
         @pl.when(owns)
         def _():
             arrived(pieces.at[:, :, lanes], rs_recv.at[g]).wait()
-            total = parts[place, :, lanes].astype(F32)
+            total = parts[place, :, lanes]
             for j in range(path_count - 1):
-                total = total + pieces[j, :, lanes].astype(F32)
+                total = total + pieces[j, :, lanes]
             total = total * (1.0 / (paths * path_count))
             finals[:, lanes] = total
             out_ref[place, :, lanes] = total
@@ -323,7 +323,7 @@
         def _():
             arrived(pieces.at[:, :, lanes].at[pl.ds(0, owners - 1)], rs_send.at[g]).wait()
             arrived(out_ref.at[pl.ds(0, owners - 1), :, lanes], ag_recv.at[g]).wait()
-            arrived(pieces.at[:, :, pl.ds(0, 2 * GROUP)], ag_send.at[g]).wait()
+            arrived(pieces.at[:, :, lanes], ag_send.at[g]).wait()
 
         @pl.when(jnp.logical_not(owns))
         def _():
@@ -359,8 +359,8 @@
                 pltpu.VMEM((5 + RIM, paths, sets), BF16),
                 pltpu.VMEM((tm_count - 1, 5 + RIM, paths, sets), BF16),
                 pltpu.VMEM((tiles, 2 * dates * 8, LANES), F32),
-                pltpu.VMEM((owners, piece_rows, sets), BF16),
-                pltpu.VMEM((path_count - 1, piece_rows, sets), BF16),
+                pltpu.VMEM((owners, piece_rows, sets), F32),
+                pltpu.VMEM((path_count - 1, piece_rows, sets), F32),
                 pltpu.VMEM((piece_rows, sets), F32),
                 dma((trades // depths[0],)),
                 dma((4,)),

time: 31.5 us -> 32.9 us (1.044)
  Pallas kernels: 29 us -> 30.4 us
    pallas_call x1, Pallas kernels: 29 us -> 30.4 us  [local(): pl.pallas_call(functools.partial(kernel, path_count, tm_count, paths, dat...]
where the time goes in v3:
time: 32.9 us; the launch traced here: 32.7 us
  Pallas kernels  30.4 us (92%)
  local copies, waits for them, and re-layouts  1.69 us (5%)
  between operations  0.64 us (2%)
    pallas_call x1, Pallas kernels, local(): pl.pallas_call(functools.partial(kernel, path_count, tm_count, paths, dat...  30.4 us
    slice x1, local copies, waits for them, and re-layouts, local(): return (out[:dates], out[dates:])  1.69 us

profile of v3, /device:TPU:0, one launch (start us, length us, event | category | flops | bytes accessed | tf_op | source)
XLA Modules:
  0.0 32.7 jit_solution(17777230247950757236)
XLA Ops:
  0.6 30.4 %shard_map.68 = f32[4,16,1024]{2,1,0:T(8,128)} custom-call(bf16[512,8192]{1,0:T(8,128)(2,1)} %bitcast.7, s32[1,8192]{1,0:T(1,128)} %bitcast.10, s32[1,1024]{1,0:T(1,128)} %bitcast.11, s32[1,1024]{1,0:T(1,128)} %bitcast.12, s32[1,1024]{1,0:T(1,128)} %bitcast.13), custom_call_target="tpu_custom_call" | custom-call | tf_op jit(solution)/shard_map/pallas_call | solution.py:347
  31.1 1.7 %fusion = (f32[2,16,1024]{2,1,0:T(8,128)}, f32[2,16,1024]{2,1,0:T(8,128)}) fusion(f32[4,16,1024]{2,1,0:T(8,128)} %shard_map.68), kind=kLoop, calls=%fused_computation | loop fusion | bytes 524288 | tf_op jit(solution)/shard_map/slice | solution.py:382
